TPU v7x, 128 devices: a whole 4x4x4 slice. The times are simulated.
128 devices in a mesh: prompt: 16 (over z, x_lo, core), ctx: 8 (over x_hi, y).
Axes of the slice: x: 4 (x_hi: 2, x_lo: 2; x = x_hi * 2 + x_lo), y: 4, z: 4, core: 2. Of those that a mesh axis runs over, the one named last changes fastest.
Arguments:
- queries: bfloat16 [65536, 16, 128], P(('prompt', 'ctx')), may hold values from -8 to 8
- keys: bfloat16 [65536, 4, 128], P(('prompt', 'ctx')), may hold values from -8 to 8
- values: bfloat16 [65536, 4, 128], P(('prompt', 'ctx')), may hold values from -6 to 6
- spans: int32 [16, 2], P('prompt'), may hold values from 1 to 3072, as said below
- partner: int32 [16], replicated, may hold values from 0 to 15, each once
Outputs:
- attended: bfloat16 [65536, 16, 128], P(('prompt', 'ctx'))
- decode_cache: bfloat16 [16, 2, 16, 8, 128, 128], P('ctx', None, 'prompt')
Inputs may be any that keep to these rules, and one draw needn't show every extreme that they name: `spans`: column 0 counts the image tokens of a prompt, from 1024 to 2048, which come first; column 1 counts the text tokens after them, 1 or more; the two sum to at most 4096, and to exactly 4096 for at least one prompt.
All inputs are finite; a program needn't handle non-finite values.
Results may differ from a plain program's by a relative error of at most 0.0041.
Values may be sent and summed in bfloat16 or wider, within the bound.
A program may use at most 64 MiB of HBM per device.

v0:
```python
import math
import jax
import jax.numpy as jnp
from jax import lax
from jax.sharding import PartitionSpec as P

far_below = -1e30


def sent_together(arrays, axis, split_dim, concat_dim, along):
    widths = [a.shape[along] for a in arrays]
    both = jnp.concatenate(arrays, axis=along)
    whole = lax.all_to_all(both, axis, split_axis=split_dim, concat_axis=concat_dim, tiled=True)
    return tuple(jnp.split(whole, [sum(widths[:k]) for k in range(1, len(widths))], axis=along))


def start_state(query):
    lead_shape = query.shape[:3]
    return (
        jnp.full(lead_shape, far_below, jnp.float32),
        jnp.zeros(lead_shape, jnp.float32),
        jnp.zeros(query.shape, jnp.float32),
    )


def key_block(progress, query, query_pos, block_keys, block_values, key_first, length):
    running_peak, row_total, accumulated = progress
    score_scale = 1.0 / math.sqrt(query.shape[-1])
    scores = (
        jnp.einsum("qgmd,kgd->qgmk", query, block_keys, preferred_element_type=jnp.float32)
        * score_scale
    )
    key_pos = key_first + lax.iota(jnp.int32, block_keys.shape[0])
    allowed = ((key_pos[None, :] <= query_pos[:, None]) & (key_pos[None, :] < length))[
        :, None, None, :
    ]
    scores = jnp.where(allowed, scores, far_below)
    new_peak = jnp.maximum(running_peak, jnp.max(scores, axis=-1))
    weights = jnp.where(allowed, jnp.exp(scores - new_peak[..., None]), 0.0)
    factor = jnp.exp(running_peak - new_peak)
    row_total = row_total * factor + jnp.sum(weights, axis=-1)
    accumulated = accumulated * factor[..., None] + jnp.einsum(
        "qgmk,kgd->qgmd",
        weights.astype(jnp.bfloat16),
        block_values,
        preferred_element_type=jnp.float32,
    )
    return (new_peak, row_total, accumulated)


def fold_keys(
    progress, query, query_pos, query_last, all_keys, all_values, key_start, length, limit
):
    key_step = math.gcd(all_keys.shape[0], limit)
    block_count = all_keys.shape[0] // key_step
    key_blocks = all_keys.reshape(block_count, key_step, all_keys.shape[1], all_keys.shape[2])
    value_blocks = all_values.reshape(
        block_count, key_step, all_values.shape[1], all_values.shape[2]
    )

    def visit_block(carried, block_item):
        block_keys, block_values, block_index = block_item
        key_first = key_start + block_index * key_step
        needed = (key_first < length) & (key_first <= query_last)
        carried = lax.cond(
            needed,
            lambda held: key_block(
                held, query, query_pos, block_keys, block_values, key_first, length
            ),
            lambda held: held,
            carried,
        )
        return (carried, None)

    progress, ignored = lax.scan(
        visit_block, progress, (key_blocks, value_blocks, jnp.arange(block_count, dtype=jnp.int32))
    )
    return progress


def finish(progress, query_pos, length):
    running_peak, row_total, accumulated = progress
    mixture = accumulated / row_total[..., None]
    mixture = jnp.where((query_pos < length)[:, None, None, None], mixture, 0.0)
    return mixture.reshape(
        mixture.shape[0], mixture.shape[1] * mixture.shape[2], mixture.shape[3]
    ).astype(jnp.bfloat16)


def per_device(queries, keys, values, spans, partner):
    tok_rows, head_count, head_width = queries.shape
    kv_heads = keys.shape[1]
    blocks = lax.axis_size("ctx")
    ctx_index = lax.axis_index("ctx")
    length = spans[0, 0] + spans[0, 1]
    stripes = lax.axis_size("prompt") // kv_heads
    live_rows = (ctx_index * tok_rows + lax.iota(jnp.int32, tok_rows) < length)[:, None, None]
    handoff = jnp.stack(
        [
            jnp.where(live_rows, keys, jnp.zeros_like(keys)),
            jnp.where(live_rows, values, jnp.zeros_like(values)),
        ]
    )
    handoff = handoff.reshape(1, 2, tok_rows // stripes, stripes * kv_heads, head_width)
    handoff = lax.all_to_all(handoff, "prompt", split_axis=3, concat_axis=0, tiled=True)
    handoff = jnp.take(handoff, partner, axis=0)
    handoff = handoff.reshape(handoff.shape[0], 2, 1, 1, tok_rows // stripes, head_width)
    handoff = lax.all_to_all(handoff, "ctx", split_axis=0, concat_axis=3, tiled=True)
    head_share = head_count // blocks
    copies = max(1, blocks // kv_heads)
    own_kv = kv_heads * copies // blocks
    query_split = queries.reshape(tok_rows, blocks, head_share, head_width)
    key_split = jnp.repeat(keys, copies, axis=1).reshape(tok_rows, blocks, own_kv, head_width)
    value_split = jnp.repeat(values, copies, axis=1).reshape(tok_rows, blocks, own_kv, head_width)
    query_all, key_all, value_all = sent_together(
        (query_split, key_split, value_split), "ctx", 1, 0, 2
    )
    sequence = blocks * tok_rows
    key_all = key_all.reshape(sequence, own_kv, head_width)
    value_all = value_all.reshape(sequence, own_kv, head_width)
    query_block = math.gcd(sequence, 2048)
    block_count = sequence // query_block
    query_blocks = query_all.reshape(
        block_count, query_block, own_kv, head_share // own_kv, head_width
    )

    def one_block(block_item):
        query_part, block_index = block_item
        query_pos = block_index * query_block + lax.iota(jnp.int32, query_block)
        query_last = block_index * query_block + query_block - 1
        progress = fold_keys(
            start_state(query_part),
            query_part,
            query_pos,
            query_last,
            key_all,
            value_all,
            0,
            length,
            1024,
        )
        return finish(progress, query_pos, length)

    finished = lax.map(one_block, (query_blocks, jnp.arange(block_count, dtype=jnp.int32)))
    finished = finished.reshape(blocks, tok_rows, head_share, head_width)
    attended = lax.all_to_all(finished, "ctx", split_axis=0, concat_axis=2, tiled=True).reshape(
        tok_rows, head_count, head_width
    )
    return (attended, handoff)


def solution(mesh):
    placed = (
        P(("prompt", "ctx"), None, None),
        P(("prompt", "ctx"), None, None),
        P(("prompt", "ctx"), None, None),
        P("prompt", None),
        P(),
    )
    return jax.shard_map(
        per_device,
        mesh=mesh,
        in_specs=placed,
        out_specs=(P(("prompt", "ctx"), None, None), P("ctx", None, "prompt", None, None, None)),
        check_vma=False,
    )
```

profile of v0, /device:TPU:32, one launch (start us, length us, event | category | flops | bytes accessed | tf_op | source)
XLA Modules:
  0.0 266.5 jit_solution(13143654870239620445)
XLA Ops:
  3.3 3.3 %broadcast_select_fusion.1 = (bf16[512,4,128]{2,1,0:T(4,128)(2,1)S(1)}, bf16[512,4,128]{2,1,0:T(4,128)(2,1)S(1)}) fusion(bf16[512,4,128]{2,1,0:T(4,128)(2,1)} %param.12, pred[512]{0:T(512)(128)(4,1)S(1)} %add_compare_fusion.1, bf16[512,4,128]{2,1,0:T(4,128)(2,1)} %param.13), kind=kLoop, calls=%fused_computation.41 | loop fusion | flops 524288 | bytes 2097664 | tf_op jit(solution)/shard_map/jit(_where)/select_n | solution.py:100
  7.9 6.4 %all-to-all-start.2 = ((bf16[1,2,128,16,128]{4,2,1,0,3:T(8,128)(2,1)}), bf16[1,2,128,16,128]{4,2,1,0,3:T(8,128)(2,1)S(1)}, u32[]{:S(2)}, u32[]{:S(2)}) async-start(bf16[1,2,128,16,128]{4,2,1,0,3:T(8,128)(2,1)} %copy.43), calls=%async_computation.2 | async-start | bytes 2097152 | tf_op jit(solution)/shard_map/all_to_all | solution.py:105
  14.4 2.1 copy.34
  16.9 2.2 pad_maximum_fusion
  19.1 9.1 %all-to-all-done.2 = bf16[1,2,128,16,128]{4,2,1,0,3:T(8,128)(2,1)S(1)} async-done(((bf16[1,2,128,16,128]{4,2,1,0,3:T(8,128)(2,1)}), bf16[1,2,128,16,128]{4,2,1,0,3:T(8,128)(2,1)S(1)}, u32[]{:S(2)}, u32[]{:S(2)}) %all-to-all-start.2) | async-done | bytes 1048608 | tf_op jit(solution)/shard_map/all_to_all | solution.py:105
  28.2 6.6 %all-to-all-start = ((bf16[512,8,4,128]{3,0,2,1:T(8,128)(2,1)}), bf16[512,8,4,128]{3,0,2,1:T(8,128)(2,1)}, u32[]{:S(2)}, u32[]{:S(2)}) async-start(bf16[512,8,4,128]{3,0,2,1:T(8,128)(2,1)} %pad_maximum_fusion), calls=%async_computation | async-start | bytes 8388608 | tf_op jit(solution)/shard_map/all_to_all | solution.py:13
  36.8 47.2 %all-to-all-done = bf16[512,8,4,128]{3,0,2,1:T(8,128)(2,1)} async-done(((bf16[512,8,4,128]{3,0,2,1:T(8,128)(2,1)}), bf16[512,8,4,128]{3,0,2,1:T(8,128)(2,1)}, u32[]{:S(2)}, u32[]{:S(2)}) %all-to-all-start) | async-done | bytes 4194336 | tf_op jit(solution)/shard_map/all_to_all | solution.py:13
  84.0 4.8 %all-to-all-start.3 = ((bf16[16,2,1,1,128,128]{5,4,1,3,2,0:T(8,128)(2,1)}), bf16[16,2,1,1,128,128]{5,4,1,3,2,0:T(8,128)(2,1)}, u32[]{:S(2)}, u32[]{:S(2)}) async-start(bf16[16,2,1,1,128,128]{5,4,1,3,2,0:T(8,128)(2,1)} %fusion.28), calls=%async_computation.3 | async-start | bytes 2097152 | tf_op jit(solution)/shard_map/all_to_all | solution.py:108
  88.8 2.5 copy.39
  94.2 133.3 %while.54 = (s32[]{:T(128)}, bf16[2,2048,2,128]{3,1,0,2:T(8,128)(2,1)}, s32[2]{0:T(128)S(1)}, s32[]{:T(128)}, bf16[4096,1,1,128]{3,0,2,1:T(8,128)(2,1)}, /*index...) while((s32[]{:T(128)}, ...), condition=%wide.region_7.8_spmd, body=%wide.region_0.7_spmd.sunk | while | flops 2208846848 | bytes 78479512 | solution.py:144
  96.9 2.3 copy.53
  99.4 41.4 %while.55 = (s32[]{:T(128)}, f32[2048,1,2]{0,2,1:T(2,128)S(1)}, f32[2048,1,2]{0,2,1:T(2,128)S(1)}, f32[2048,1,2,128]{0,3,2,1:T(8,128)S(1)}, s32[4]{0:T(128)S(1)}...) while((s32[]{:T(128)}, f32[2048,1,2]{0,2,1:T(2,128)S(1)}, ...), condition=%wide.region_6.6_spmd.clone, body=%wide.region_1.5_spmd.clone.sunk | while | flops 2207269888 | bytes 64793936 | solution.py:75
  100.7 18.1 %conditional.3 = ((f32[2048,1,2]{0,2,1:T(2,128)S(1)}, f32[2048,1,2]{0,2,1:T(2,128)S(1)}, f32[2048,1,2,128]{0,3,2,1:T(8,128)S(1)})) conditional(s32[]{:T(128)} %convert_element_type.42, (f32[2048,1,2]{0,2,1:T(2,128)S(1)}, f32[2048,1,2]{0,2,1:T(2,128)S(1)}, f32[2048,1,2,128]{0,3,2,1:T(8,128)S(1)}) %tuple.87, (s32[]{:T(128)}, s32[]{:T(128)}, s32[]{:T(128)}, ...), branch_computations={%region_2.1_spmd, %region_3.4_spmd} | conditional | flops 2207269888 | bytes 64785456 | solution.py:65
  100.8 1.7 compare_and_fusion
  102.5 4.6 %fusion.2 = (f32[2048,2]{0,1:T(2,128)S(1)}, f32[1024,2048,2]{1,0,2:T(8,128)S(1)}) fusion(pred[2048,1024]{0,1:T(8,128)(4,1)S(1)} %compare_and_fusion, bf16[2048,1,2,128]{3,0,2,1:T(8,128)(2,1)S(1)} %get-tuple-element.259, bf16[4,1024,1,128]{3,1,2,0:T(8,128)(2,1)} %get-tuple-element.257, s32[]{:T(128)} %get-tuple-element.258), kind=kOutput, calls=%fused_computation.4 | convolution fusion | flops 1086320640 | bytes 20201984 | tf_op jit(solution)/shard_map/while/body/eval_jaxpr/while/body/eval_jaxpr/cond/branch_1_fun/qgmd,kgd->qgmk/dot_general | solution.py:30
  107.1 7.1 %fusion.12 = f32[2048,1,2,128]{0,3,2,1:T(8,128)S(1)} fusion(f32[1024,2048,2]{1,0,2:T(8,128)S(1)} %get-tuple-element.429, f32[2048,2]{0,1:T(2,128)S(1)} %bitcast.119, pred[2048,1024]{0,1:T(8,128)(4,1)S(1)} %compare_and_fusion, f32[2048,1,2,128]{0,3,2,1:T(8,128)S(1)} %get-tuple-element.261, f32[2048,2]{0,1:T(2,128)S(1)} %get-tuple-element.426, ...), kind=kOutput, calls=%fused_computation.12 | convolution fusion | flops 1095761920 | bytes 23364096 | tf_op jit(solution)/shard_map/while/body/eval_jaxpr/while/body/eval_jaxpr/cond/branch_1_fun/qgmk,kgd->qgmd/dot_general | solution.py:42
  114.2 4.5 %fusion.4 = f32[2048,2]{0,1:T(2,128)S(1)} fusion(f32[1024,2048,2]{1,0,2:T(8,128)S(1)} %get-tuple-element.429, f32[2048,2]{0,1:T(2,128)S(1)} %bitcast.120, pred[2048,1024]{0,1:T(8,128)(4,1)S(1)} %compare_and_fusion), kind=kLoop, calls=%fused_computation.6 | loop fusion | flops 20967424 | bytes 18907136 | tf_op jit(solution)/shard_map/while/body/eval_jaxpr/while/body/eval_jaxpr/cond/branch_1_fun/reduce_sum | solution.py:41
  120.1 18.1 %conditional.3 = ((f32[2048,1,2]{0,2,1:T(2,128)S(1)}, f32[2048,1,2]{0,2,1:T(2,128)S(1)}, f32[2048,1,2,128]{0,3,2,1:T(8,128)S(1)})) conditional(s32[]{:T(128)} %convert_element_type.42, (f32[2048,1,2]{0,2,1:T(2,128)S(1)}, f32[2048,1,2]{0,2,1:T(2,128)S(1)}, f32[2048,1,2,128]{0,3,2,1:T(8,128)S(1)}) %tuple.87, (s32[]{:T(128)}, s32[]{:T(128)}, s32[]{:T(128)}, ...), branch_computations={%region_2.1_spmd, %region_3.4_spmd} | conditional | flops 2207269888 | bytes 64785456 | solution.py:65
  120.1 1.7 compare_and_fusion
  121.8 4.6 %fusion.2 = (f32[2048,2]{0,1:T(2,128)S(1)}, f32[1024,2048,2]{1,0,2:T(8,128)S(1)}) fusion(pred[2048,1024]{0,1:T(8,128)(4,1)S(1)} %compare_and_fusion, bf16[2048,1,2,128]{3,0,2,1:T(8,128)(2,1)S(1)} %get-tuple-element.259, bf16[4,1024,1,128]{3,1,2,0:T(8,128)(2,1)} %get-tuple-element.257, s32[]{:T(128)} %get-tuple-element.258), kind=kOutput, calls=%fused_computation.4 | convolution fusion | flops 1086320640 | bytes 20201984 | tf_op jit(solution)/shard_map/while/body/eval_jaxpr/while/body/eval_jaxpr/cond/branch_1_fun/qgmd,kgd->qgmk/dot_general | solution.py:30
  126.5 7.1 %fusion.12 = f32[2048,1,2,128]{0,3,2,1:T(8,128)S(1)} fusion(f32[1024,2048,2]{1,0,2:T(8,128)S(1)} %get-tuple-element.429, f32[2048,2]{0,1:T(2,128)S(1)} %bitcast.119, pred[2048,1024]{0,1:T(8,128)(4,1)S(1)} %compare_and_fusion, f32[2048,1,2,128]{0,3,2,1:T(8,128)S(1)} %get-tuple-element.261, f32[2048,2]{0,1:T(2,128)S(1)} %get-tuple-element.426, ...), kind=kOutput, calls=%fused_computation.12 | convolution fusion | flops 1095761920 | bytes 23364096 | tf_op jit(solution)/shard_map/while/body/eval_jaxpr/while/body/eval_jaxpr/cond/branch_1_fun/qgmk,kgd->qgmd/dot_general | solution.py:42
  133.6 4.5 %fusion.4 = f32[2048,2]{0,1:T(2,128)S(1)} fusion(f32[1024,2048,2]{1,0,2:T(8,128)S(1)} %get-tuple-element.429, f32[2048,2]{0,1:T(2,128)S(1)} %bitcast.120, pred[2048,1024]{0,1:T(8,128)(4,1)S(1)} %compare_and_fusion), kind=kLoop, calls=%fused_computation.6 | loop fusion | flops 20967424 | bytes 18907136 | tf_op jit(solution)/shard_map/while/body/eval_jaxpr/while/body/eval_jaxpr/cond/branch_1_fun/reduce_sum | solution.py:41
  145.4 2.3 copy.53
  148.0 77.5 %while.55 = (s32[]{:T(128)}, f32[2048,1,2]{0,2,1:T(2,128)S(1)}, f32[2048,1,2]{0,2,1:T(2,128)S(1)}, f32[2048,1,2,128]{0,3,2,1:T(8,128)S(1)}, s32[4]{0:T(128)S(1)}...) while((s32[]{:T(128)}, f32[2048,1,2]{0,2,1:T(2,128)S(1)}, ...), condition=%wide.region_6.6_spmd.clone, body=%wide.region_1.5_spmd.clone.sunk | while | flops 2207269888 | bytes 64793936 | solution.py:75
  149.3 18.0 %conditional.3 = ((f32[2048,1,2]{0,2,1:T(2,128)S(1)}, f32[2048,1,2]{0,2,1:T(2,128)S(1)}, f32[2048,1,2,128]{0,3,2,1:T(8,128)S(1)})) conditional(s32[]{:T(128)} %convert_element_type.42, (f32[2048,1,2]{0,2,1:T(2,128)S(1)}, f32[2048,1,2]{0,2,1:T(2,128)S(1)}, f32[2048,1,2,128]{0,3,2,1:T(8,128)S(1)}) %tuple.87, (s32[]{:T(128)}, s32[]{:T(128)}, s32[]{:T(128)}, ...), branch_computations={%region_2.1_spmd, %region_3.4_spmd} | conditional | flops 2207269888 | bytes 64785456 | solution.py:65
  149.3 1.7 compare_and_fusion
  151.0 4.6 %fusion.2 = (f32[2048,2]{0,1:T(2,128)S(1)}, f32[1024,2048,2]{1,0,2:T(8,128)S(1)}) fusion(pred[2048,1024]{0,1:T(8,128)(4,1)S(1)} %compare_and_fusion, bf16[2048,1,2,128]{3,0,2,1:T(8,128)(2,1)S(1)} %get-tuple-element.259, bf16[4,1024,1,128]{3,1,2,0:T(8,128)(2,1)} %get-tuple-element.257, s32[]{:T(128)} %get-tuple-element.258), kind=kOutput, calls=%fused_computation.4 | convolution fusion | flops 1086320640 | bytes 20201984 | tf_op jit(solution)/shard_map/while/body/eval_jaxpr/while/body/eval_jaxpr/cond/branch_1_fun/qgmd,kgd->qgmk/dot_general | solution.py:30
  155.7 7.1 %fusion.12 = f32[2048,1,2,128]{0,3,2,1:T(8,128)S(1)} fusion(f32[1024,2048,2]{1,0,2:T(8,128)S(1)} %get-tuple-element.429, f32[2048,2]{0,1:T(2,128)S(1)} %bitcast.119, pred[2048,1024]{0,1:T(8,128)(4,1)S(1)} %compare_and_fusion, f32[2048,1,2,128]{0,3,2,1:T(8,128)S(1)} %get-tuple-element.261, f32[2048,2]{0,1:T(2,128)S(1)} %get-tuple-element.426, ...), kind=kOutput, calls=%fused_computation.12 | convolution fusion | flops 1095761920 | bytes 23364096 | tf_op jit(solution)/shard_map/while/body/eval_jaxpr/while/body/eval_jaxpr/cond/branch_1_fun/qgmk,kgd->qgmd/dot_general | solution.py:42
  162.8 4.5 %fusion.4 = f32[2048,2]{0,1:T(2,128)S(1)} fusion(f32[1024,2048,2]{1,0,2:T(8,128)S(1)} %get-tuple-element.429, f32[2048,2]{0,1:T(2,128)S(1)} %bitcast.120, pred[2048,1024]{0,1:T(8,128)(4,1)S(1)} %compare_and_fusion), kind=kLoop, calls=%fused_computation.6 | loop fusion | flops 20967424 | bytes 18907136 | tf_op jit(solution)/shard_map/while/body/eval_jaxpr/while/body/eval_jaxpr/cond/branch_1_fun/reduce_sum | solution.py:41
  168.6 18.1 %conditional.3 = ((f32[2048,1,2]{0,2,1:T(2,128)S(1)}, f32[2048,1,2]{0,2,1:T(2,128)S(1)}, f32[2048,1,2,128]{0,3,2,1:T(8,128)S(1)})) conditional(s32[]{:T(128)} %convert_element_type.42, (f32[2048,1,2]{0,2,1:T(2,128)S(1)}, f32[2048,1,2]{0,2,1:T(2,128)S(1)}, f32[2048,1,2,128]{0,3,2,1:T(8,128)S(1)}) %tuple.87, (s32[]{:T(128)}, s32[]{:T(128)}, s32[]{:T(128)}, ...), branch_computations={%region_2.1_spmd, %region_3.4_spmd} | conditional | flops 2207269888 | bytes 64785456 | solution.py:65
  168.7 1.7 compare_and_fusion
  170.4 4.6 %fusion.2 = (f32[2048,2]{0,1:T(2,128)S(1)}, f32[1024,2048,2]{1,0,2:T(8,128)S(1)}) fusion(pred[2048,1024]{0,1:T(8,128)(4,1)S(1)} %compare_and_fusion, bf16[2048,1,2,128]{3,0,2,1:T(8,128)(2,1)S(1)} %get-tuple-element.259, bf16[4,1024,1,128]{3,1,2,0:T(8,128)(2,1)} %get-tuple-element.257, s32[]{:T(128)} %get-tuple-element.258), kind=kOutput, calls=%fused_computation.4 | convolution fusion | flops 1086320640 | bytes 20201984 | tf_op jit(solution)/shard_map/while/body/eval_jaxpr/while/body/eval_jaxpr/cond/branch_1_fun/qgmd,kgd->qgmk/dot_general | solution.py:30
  175.1 7.1 %fusion.12 = f32[2048,1,2,128]{0,3,2,1:T(8,128)S(1)} fusion(f32[1024,2048,2]{1,0,2:T(8,128)S(1)} %get-tuple-element.429, f32[2048,2]{0,1:T(2,128)S(1)} %bitcast.119, pred[2048,1024]{0,1:T(8,128)(4,1)S(1)} %compare_and_fusion, f32[2048,1,2,128]{0,3,2,1:T(8,128)S(1)} %get-tuple-element.261, f32[2048,2]{0,1:T(2,128)S(1)} %get-tuple-element.426, ...), kind=kOutput, calls=%fused_computation.12 | convolution fusion | flops 1095761920 | bytes 23364096 | tf_op jit(solution)/shard_map/while/body/eval_jaxpr/while/body/eval_jaxpr/cond/branch_1_fun/qgmk,kgd->qgmd/dot_general | solution.py:42
  182.1 4.5 %fusion.4 = f32[2048,2]{0,1:T(2,128)S(1)} fusion(f32[1024,2048,2]{1,0,2:T(8,128)S(1)} %get-tuple-element.429, f32[2048,2]{0,1:T(2,128)S(1)} %bitcast.120, pred[2048,1024]{0,1:T(8,128)(4,1)S(1)} %compare_and_fusion), kind=kLoop, calls=%fused_computation.6 | loop fusion | flops 20967424 | bytes 18907136 | tf_op jit(solution)/shard_map/while/body/eval_jaxpr/while/body/eval_jaxpr/cond/branch_1_fun/reduce_sum | solution.py:41
  188.0 18.1 %conditional.3 = ((f32[2048,1,2]{0,2,1:T(2,128)S(1)}, f32[2048,1,2]{0,2,1:T(2,128)S(1)}, f32[2048,1,2,128]{0,3,2,1:T(8,128)S(1)})) conditional(s32[]{:T(128)} %convert_element_type.42, (f32[2048,1,2]{0,2,1:T(2,128)S(1)}, f32[2048,1,2]{0,2,1:T(2,128)S(1)}, f32[2048,1,2,128]{0,3,2,1:T(8,128)S(1)}) %tuple.87, (s32[]{:T(128)}, s32[]{:T(128)}, s32[]{:T(128)}, ...), branch_computations={%region_2.1_spmd, %region_3.4_spmd} | conditional | flops 2207269888 | bytes 64785456 | solution.py:65
  188.1 1.7 compare_and_fusion
  189.8 4.6 %fusion.2 = (f32[2048,2]{0,1:T(2,128)S(1)}, f32[1024,2048,2]{1,0,2:T(8,128)S(1)}) fusion(pred[2048,1024]{0,1:T(8,128)(4,1)S(1)} %compare_and_fusion, bf16[2048,1,2,128]{3,0,2,1:T(8,128)(2,1)S(1)} %get-tuple-element.259, bf16[4,1024,1,128]{3,1,2,0:T(8,128)(2,1)} %get-tuple-element.257, s32[]{:T(128)} %get-tuple-element.258), kind=kOutput, calls=%fused_computation.4 | convolution fusion | flops 1086320640 | bytes 20201984 | tf_op jit(solution)/shard_map/while/body/eval_jaxpr/while/body/eval_jaxpr/cond/branch_1_fun/qgmd,kgd->qgmk/dot_general | solution.py:30
  194.4 7.1 %fusion.12 = f32[2048,1,2,128]{0,3,2,1:T(8,128)S(1)} fusion(f32[1024,2048,2]{1,0,2:T(8,128)S(1)} %get-tuple-element.429, f32[2048,2]{0,1:T(2,128)S(1)} %bitcast.119, pred[2048,1024]{0,1:T(8,128)(4,1)S(1)} %compare_and_fusion, f32[2048,1,2,128]{0,3,2,1:T(8,128)S(1)} %get-tuple-element.261, f32[2048,2]{0,1:T(2,128)S(1)} %get-tuple-element.426, ...), kind=kOutput, calls=%fused_computation.12 | convolution fusion | flops 1095761920 | bytes 23364096 | tf_op jit(solution)/shard_map/while/body/eval_jaxpr/while/body/eval_jaxpr/cond/branch_1_fun/qgmk,kgd->qgmd/dot_general | solution.py:42
  201.5 4.5 %fusion.4 = f32[2048,2]{0,1:T(2,128)S(1)} fusion(f32[1024,2048,2]{1,0,2:T(8,128)S(1)} %get-tuple-element.429, f32[2048,2]{0,1:T(2,128)S(1)} %bitcast.120, pred[2048,1024]{0,1:T(8,128)(4,1)S(1)} %compare_and_fusion), kind=kLoop, calls=%fused_computation.6 | loop fusion | flops 20967424 | bytes 18907136 | tf_op jit(solution)/shard_map/while/body/eval_jaxpr/while/body/eval_jaxpr/cond/branch_1_fun/reduce_sum | solution.py:41
  207.4 18.1 %conditional.3 = ((f32[2048,1,2]{0,2,1:T(2,128)S(1)}, f32[2048,1,2]{0,2,1:T(2,128)S(1)}, f32[2048,1,2,128]{0,3,2,1:T(8,128)S(1)})) conditional(s32[]{:T(128)} %convert_element_type.42, (f32[2048,1,2]{0,2,1:T(2,128)S(1)}, f32[2048,1,2]{0,2,1:T(2,128)S(1)}, f32[2048,1,2,128]{0,3,2,1:T(8,128)S(1)}) %tuple.87, (s32[]{:T(128)}, s32[]{:T(128)}, s32[]{:T(128)}, ...), branch_computations={%region_2.1_spmd, %region_3.4_spmd} | conditional | flops 2207269888 | bytes 64785456 | solution.py:65
  209.1 4.6 %fusion.2 = (f32[2048,2]{0,1:T(2,128)S(1)}, f32[1024,2048,2]{1,0,2:T(8,128)S(1)}) fusion(pred[2048,1024]{0,1:T(8,128)(4,1)S(1)} %compare_and_fusion, bf16[2048,1,2,128]{3,0,2,1:T(8,128)(2,1)S(1)} %get-tuple-element.259, bf16[4,1024,1,128]{3,1,2,0:T(8,128)(2,1)} %get-tuple-element.257, s32[]{:T(128)} %get-tuple-element.258), kind=kOutput, calls=%fused_computation.4 | convolution fusion | flops 1086320640 | bytes 20201984 | tf_op jit(solution)/shard_map/while/body/eval_jaxpr/while/body/eval_jaxpr/cond/branch_1_fun/qgmd,kgd->qgmk/dot_general | solution.py:30
  213.8 7.1 %fusion.12 = f32[2048,1,2,128]{0,3,2,1:T(8,128)S(1)} fusion(f32[1024,2048,2]{1,0,2:T(8,128)S(1)} %get-tuple-element.429, f32[2048,2]{0,1:T(2,128)S(1)} %bitcast.119, pred[2048,1024]{0,1:T(8,128)(4,1)S(1)} %compare_and_fusion, f32[2048,1,2,128]{0,3,2,1:T(8,128)S(1)} %get-tuple-element.261, f32[2048,2]{0,1:T(2,128)S(1)} %get-tuple-element.426, ...), kind=kOutput, calls=%fused_computation.12 | convolution fusion | flops 1095761920 | bytes 23364096 | tf_op jit(solution)/shard_map/while/body/eval_jaxpr/while/body/eval_jaxpr/cond/branch_1_fun/qgmk,kgd->qgmd/dot_general | solution.py:42
  220.9 4.5 %fusion.4 = f32[2048,2]{0,1:T(2,128)S(1)} fusion(f32[1024,2048,2]{1,0,2:T(8,128)S(1)} %get-tuple-element.429, f32[2048,2]{0,1:T(2,128)S(1)} %bitcast.120, pred[2048,1024]{0,1:T(8,128)(4,1)S(1)} %compare_and_fusion), kind=kLoop, calls=%fused_computation.6 | loop fusion | flops 20967424 | bytes 18907136 | tf_op jit(solution)/shard_map/while/body/eval_jaxpr/while/body/eval_jaxpr/cond/branch_1_fun/reduce_sum | solution.py:41
  227.4 3.1 %copy.42 = bf16[8,512,2,128]{3,1,2,0:T(8,128)(2,1)} copy(bf16[8,512,2,128]{3,1,0,2:T(8,128)(2,1)} %bitcast.129) | data formatting | bytes 4194304 | tf_op jit(solution)/shard_map/reshape | solution.py:145
  230.6 7.2 %all-to-all-start.1 = ((bf16[8,512,2,128]{3,1,2,0:T(8,128)(2,1)}), bf16[8,512,2,128]{3,1,2,0:T(8,128)(2,1)S(1)}, u32[]{:S(2)}, u32[]{:S(2)}) async-start(bf16[8,512,2,128]{3,1,2,0:T(8,128)(2,1)} %copy.42), calls=%async_computation.1 | async-start | bytes 4194304 | tf_op jit(solution)/shard_map/all_to_all | solution.py:146
  237.8 2.3 copy.46
  240.1 23.7 %all-to-all-done.1 = bf16[8,512,2,128]{3,1,2,0:T(8,128)(2,1)S(1)} async-done(((bf16[8,512,2,128]{3,1,2,0:T(8,128)(2,1)}), bf16[8,512,2,128]{3,1,2,0:T(8,128)(2,1)S(1)}, u32[]{:S(2)}, u32[]{:S(2)}) %all-to-all-start.1) | async-done | bytes 2097184 | tf_op jit(solution)/shard_map/all_to_all | solution.py:146
  263.8 2.7 %copy.45 = bf16[512,16,128]{2,1,0:T(8,128)(2,1)} copy(bf16[512,16,128]{2,0,1:T(8,128)(2,1)S(1)} %bitcast.124) | data formatting | bytes 4194304
  (99 shorter events, 23.7 us)
Async XLA Ops:
  3.3 11.0 %copy-start = (bf16[512,4,128]{2,1,0:T(4,128)(2,1)S(1)}, bf16[512,4,128]{2,1,0:T(4,128)(2,1)}, u32[]{:S(2)}) copy-start(bf16[512,4,128]{2,1,0:T(4,128)(2,1)} %param.12) | copy-start | bytes 1572868
  6.5 7.8 %copy-start.1 = (bf16[512,4,128]{2,1,0:T(4,128)(2,1)S(1)}, bf16[512,4,128]{2,1,0:T(4,128)(2,1)}, u32[]{:S(2)}) copy-start(bf16[512,4,128]{2,1,0:T(4,128)(2,1)} %param.13) | copy-start | bytes 1572868
  7.9 20.3 %all-to-all-start.2 = ((bf16[1,2,128,16,128]{4,2,1,0,3:T(8,128)(2,1)}), bf16[1,2,128,16,128]{4,2,1,0,3:T(8,128)(2,1)S(1)}, u32[]{:S(2)}, u32[]{:S(2)}) async-start(bf16[1,2,128,16,128]{4,2,1,0,3:T(8,128)(2,1)} %copy.43), calls=%async_computation.2 | async-start | bytes 2097152 | tf_op jit(solution)/shard_map/all_to_all | solution.py:105
  19.1 15.7 %copy-start.2 = (s32[16]{0:T(128)S(1)}, s32[16]{0:T(128)}, u32[]{:S(2)}) copy-start(s32[16]{0:T(128)} %param.15) | copy-start | bytes 196
  28.2 55.9 %all-to-all-start = ((bf16[512,8,4,128]{3,0,2,1:T(8,128)(2,1)}), bf16[512,8,4,128]{3,0,2,1:T(8,128)(2,1)}, u32[]{:S(2)}, u32[]{:S(2)}) async-start(bf16[512,8,4,128]{3,0,2,1:T(8,128)(2,1)} %pad_maximum_fusion), calls=%async_computation | async-start | bytes 8388608 | tf_op jit(solution)/shard_map/all_to_all | solution.py:13
  84.0 146.5 %all-to-all-start.3 = ((bf16[16,2,1,1,128,128]{5,4,1,3,2,0:T(8,128)(2,1)}), bf16[16,2,1,1,128,128]{5,4,1,3,2,0:T(8,128)(2,1)}, u32[]{:S(2)}, u32[]{:S(2)}) async-start(bf16[16,2,1,1,128,128]{5,4,1,3,2,0:T(8,128)(2,1)} %fusion.28), calls=%async_computation.3 | async-start | bytes 2097152 | tf_op jit(solution)/shard_map/all_to_all | solution.py:108
  230.6 33.2 %all-to-all-start.1 = ((bf16[8,512,2,128]{3,1,2,0:T(8,128)(2,1)}), bf16[8,512,2,128]{3,1,2,0:T(8,128)(2,1)S(1)}, u32[]{:S(2)}, u32[]{:S(2)}) async-start(bf16[8,512,2,128]{3,1,2,0:T(8,128)(2,1)} %copy.42), calls=%async_computation.1 | async-start | bytes 4194304 | tf_op jit(solution)/shard_map/all_to_all | solution.py:146
where the time goes:
time: 268 us; the launch traced here: 266 us
  waiting for transfers between devices  80 us (30%)
  matrix products  70.1 us (26%)
  other arithmetic  45.1 us (17%)
  local copies, waits for them, and re-layouts  36.9 us (14%)
  starting transfers between devices  25 us (9%)
  loops' own time  7.36 us (3%)
    all_to_all x1, waiting for transfers between devices, sent_together(): lax.all_to_all(both, axis, split_axis=split_dim, concat_axis=concat_dim,...  47.2 us
    dot_general x6, matrix products, key_block(): jnp.einsum('qgmk,kgd->qgmd', weights.astype(jnp.bfloat16), block_values,...  42.4 us
    dot_general x6, matrix products, key_block(): jnp.einsum('qgmd,kgd->qgmk', query, block_keys, preferred_element_type=jn...  27.7 us
    reduce_sum x6, other arithmetic, key_block(): row_total = row_total * factor + jnp.sum(weights, axis=-1)  27.1 us
    all_to_all x1, waiting for transfers between devices, per_device(): lax.all_to_all(finished, 'ctx', split_axis=0, concat_axis=2, tiled=True)  23.7 us
    and x6, other arithmetic, key_block(): (key_pos[None, :] <= query_pos[:, None]) & (key_pos[None, :] < length)  10.2 us
    all_to_all x1, waiting for transfers between devices, per_device(): lax.all_to_all(handoff, 'prompt', split_axis=3, concat_axis=0, tiled=True)  9.08 us
    unnamed x11, local copies, waits for them, and re-layouts  7.27 us
  transfers between devices with their start and end apart: 4, of which 3 were waited for; matrix products, arithmetic and copies ran while one was open for 54% of the time, Pallas kernels for 0%

commit v1 on v0

--- a/solution.py
+++ b/solution.py
@@ -102,7 +102,12 @@
         ]
     )
     handoff = handoff.reshape(1, 2, tok_rows // stripes, stripes * kv_heads, head_width)
-    handoff = lax.all_to_all(handoff, "prompt", split_axis=3, concat_axis=0, tiled=True)
+    handoff = jnp.concatenate(
+        lax.all_to_all(
+            jnp.stack(jnp.split(handoff, lax.axis_size("prompt"), axis=3)), "prompt", 0, 0
+        ),
+        axis=0,
+    )
     handoff = jnp.take(handoff, partner, axis=0)
     handoff = handoff.reshape(handoff.shape[0], 2, 1, 1, tok_rows // stripes, head_width)
     handoff = lax.all_to_all(handoff, "ctx", split_axis=0, concat_axis=3, tiled=True)

time: 268 us -> 279 us (1.041)
  local copies, waits for them, and re-layouts: 36.9 us -> 45.8 us
    unnamed x11 -> x26, local copies, waits for them, and re-layouts: 7.27 us -> 16.9 us
  transfers between devices with their start and end apart: 4 -> 4, of which waited for: 3 -> 3; matrix products, arithmetic and copies ran while one was open for 54% -> 52% of each run, Pallas kernels for 0% -> 0%
where the time goes in v1:
time: 279 us; the launch traced here: 278 us
  waiting for transfers between devices  80 us (29%)
  matrix products  70.1 us (25%)
  other arithmetic  47.7 us (17%)
  local copies, waits for them, and re-layouts  45.8 us (16%)
  starting transfers between devices  25 us (9%)
  loops' own time  7.26 us (3%)
    all_to_all x1, waiting for transfers between devices, sent_together(): lax.all_to_all(both, axis, split_axis=split_dim, concat_axis=concat_dim,...  47.2 us
    dot_general x6, matrix products, key_block(): jnp.einsum('qgmk,kgd->qgmd', weights.astype(jnp.bfloat16), block_values,...  42.4 us
    dot_general x6, matrix products, key_block(): jnp.einsum('qgmd,kgd->qgmk', query, block_keys, preferred_element_type=jn...  27.7 us
    reduce_sum x6, other arithmetic, key_block(): row_total = row_total * factor + jnp.sum(weights, axis=-1)  27.1 us
    all_to_all x1, waiting for transfers between devices, per_device(): lax.all_to_all(finished, 'ctx', split_axis=0, concat_axis=2, tiled=True)  23.7 us
    unnamed x26, local copies, waits for them, and re-layouts  16.9 us
    and x6, other arithmetic, key_block(): (key_pos[None, :] <= query_pos[:, None]) & (key_pos[None, :] < length)  10.2 us
    all_to_all x1, waiting for transfers between devices, per_device(): lax.all_to_all(jnp.stack(jnp.split(handoff, lax.axis_size('prompt'), axis...  9.07 us
  transfers between devices with their start and end apart: 4, of which 3 were waited for; matrix products, arithmetic and copies ran while one was open for 52% of the time, Pallas kernels for 0%

profile of v1, /device:TPU:32, one launch (start us, length us, event | category | flops | bytes accessed | tf_op | source)
XLA Modules:
  0.0 277.8 jit_solution(15981988160392137673)
XLA Ops:
  3.3 3.2 %broadcast_select_fusion = (bf16[512,4,128]{2,1,0:T(4,128)(2,1)S(1)}, bf16[512,4,128]{2,1,0:T(4,128)(2,1)S(1)}) fusion(bf16[512,4,128]{2,1,0:T(4,128)(2,1)} %param.13, pred[512]{0:T(512)(128)(4,1)S(1)} %add_compare_fusion.1, bf16[512,4,128]{2,1,0:T(4,128)(2,1)} %param.12), kind=kLoop, calls=%fused_computation.69 | loop fusion | flops 524288 | bytes 2097664 | tf_op jit(solution)/shard_map/jit(_where)/select_n | solution.py:101
  19.5 6.4 %all-to-all-start.2 = ((bf16[16,1,2,128,1,128]{5,3,2,4,1,0:T(8,128)(2,1)}), bf16[16,1,2,128,1,128]{5,3,2,4,1,0:T(8,128)(2,1)S(1)}, u32[]{:S(2)}, u32[]{:S(2)}) async-start(bf16[16,1,2,128,1,128]{5,3,2,4,1,0:T(8,128)(2,1)} %bitcast_dynamic-update-slice_fusion), calls=%async_computation.2 | async-start | bytes 2097152 | tf_op jit(solution)/shard_map/all_to_all | solution.py:106
  26.0 2.1 copy.302
  28.5 2.2 pad_maximum_fusion
  30.7 9.1 %all-to-all-done.2 = bf16[16,1,2,128,1,128]{5,3,2,4,1,0:T(8,128)(2,1)S(1)} async-done(((bf16[16,1,2,128,1,128]{5,3,2,4,1,0:T(8,128)(2,1)}), bf16[16,1,2,128,1,128]{5,3,2,4,1,0:T(8,128)(2,1)S(1)}, u32[]{:S(2)}, u32[]{:S(2)}) %all-to-all-start.2) | async-done | bytes 1048608 | tf_op jit(solution)/shard_map/all_to_all | solution.py:106
  39.8 6.6 %all-to-all-start = ((bf16[512,8,4,128]{3,0,2,1:T(8,128)(2,1)}), bf16[512,8,4,128]{3,0,2,1:T(8,128)(2,1)}, u32[]{:S(2)}, u32[]{:S(2)}) async-start(bf16[512,8,4,128]{3,0,2,1:T(8,128)(2,1)} %pad_maximum_fusion), calls=%async_computation | async-start | bytes 8388608 | tf_op jit(solution)/shard_map/all_to_all | solution.py:13
  48.4 47.2 %all-to-all-done = bf16[512,8,4,128]{3,0,2,1:T(8,128)(2,1)} async-done(((bf16[512,8,4,128]{3,0,2,1:T(8,128)(2,1)}), bf16[512,8,4,128]{3,0,2,1:T(8,128)(2,1)}, u32[]{:S(2)}, u32[]{:S(2)}) %all-to-all-start) | async-done | bytes 4194336 | tf_op jit(solution)/shard_map/all_to_all | solution.py:13
  95.6 4.8 %all-to-all-start.3 = ((bf16[16,2,1,1,128,128]{5,4,1,3,2,0:T(8,128)(2,1)}), bf16[16,2,1,1,128,128]{5,4,1,3,2,0:T(8,128)(2,1)}, u32[]{:S(2)}, u32[]{:S(2)}) async-start(bf16[16,2,1,1,128,128]{5,4,1,3,2,0:T(8,128)(2,1)} %fusion.28), calls=%async_computation.3 | async-start | bytes 2097152 | tf_op jit(solution)/shard_map/all_to_all | solution.py:113
  100.4 2.5 copy.307
  105.8 133.0 %while.54 = (s32[]{:T(128)}, bf16[2,2048,2,128]{3,1,0,2:T(8,128)(2,1)}, s32[2]{0:T(128)S(1)}, s32[]{:T(128)}, bf16[4096,1,1,128]{3,0,2,1:T(8,128)(2,1)}, /*index...) while((s32[]{:T(128)}, ...), condition=%wide.region_7.8_spmd, body=%wide.region_0.7_spmd.sunk | while | flops 2208846848 | bytes 78479024 | solution.py:149
  108.3 2.3 copy.352
  110.8 41.4 %while.55 = (s32[]{:T(128)}, f32[2048,1,2]{0,2,1:T(2,128)S(1)}, f32[2048,1,2]{0,2,1:T(2,128)S(1)}, f32[2048,1,2,128]{0,3,2,1:T(8,128)S(1)}, s32[4]{0:T(128)S(1)}...) while((s32[]{:T(128)}, f32[2048,1,2]{0,2,1:T(2,128)S(1)}, ...), condition=%wide.region_6.6_spmd.clone, body=%wide.region_1.5_spmd.clone.sunk | while | flops 2207269888 | bytes 64793944 | solution.py:75
  112.2 18.1 %conditional.3 = ((f32[2048,1,2]{0,2,1:T(2,128)S(1)}, f32[2048,1,2]{0,2,1:T(2,128)S(1)}, f32[2048,1,2,128]{0,3,2,1:T(8,128)S(1)})) conditional(s32[]{:T(128)} %convert_element_type.42, (f32[2048,1,2]{0,2,1:T(2,128)S(1)}, f32[2048,1,2]{0,2,1:T(2,128)S(1)}, f32[2048,1,2,128]{0,3,2,1:T(8,128)S(1)}) %tuple.146, (s32[]{:T(128)}, s32[]{:T(128)}, s32[]{:T(128)}, ...), branch_computations={%region_2.1_spmd, %region_3.4_spmd} | conditional | flops 2207269888 | bytes 64785456 | solution.py:65
  112.2 1.7 compare_and_fusion
  113.9 4.6 %fusion.2 = (f32[2048,2]{0,1:T(2,128)S(1)}, f32[1024,2048,2]{1,0,2:T(8,128)S(1)}) fusion(pred[2048,1024]{0,1:T(8,128)(4,1)S(1)} %compare_and_fusion, bf16[2048,1,2,128]{3,0,2,1:T(8,128)(2,1)S(1)} %get-tuple-element.259, bf16[4,1024,1,128]{3,1,2,0:T(8,128)(2,1)} %get-tuple-element.257, s32[]{:T(128)} %get-tuple-element.258), kind=kOutput, calls=%fused_computation.4 | convolution fusion | flops 1086320640 | bytes 20201984 | tf_op jit(solution)/shard_map/while/body/eval_jaxpr/while/body/eval_jaxpr/cond/branch_1_fun/qgmd,kgd->qgmk/dot_general | solution.py:30
  118.6 4.5 %fusion.4 = f32[2048,2]{0,1:T(2,128)S(1)} fusion(f32[1024,2048,2]{1,0,2:T(8,128)S(1)} %get-tuple-element.729, f32[2048,2]{0,1:T(2,128)S(1)} %bitcast.147, pred[2048,1024]{0,1:T(8,128)(4,1)S(1)} %compare_and_fusion), kind=kLoop, calls=%fused_computation.6 | loop fusion | flops 20967424 | bytes 18907136 | tf_op jit(solution)/shard_map/while/body/eval_jaxpr/while/body/eval_jaxpr/cond/branch_1_fun/reduce_sum | solution.py:41
  123.1 7.1 %fusion.12 = f32[2048,1,2,128]{0,3,2,1:T(8,128)S(1)} fusion(f32[1024,2048,2]{1,0,2:T(8,128)S(1)} %get-tuple-element.729, f32[2048,2]{0,1:T(2,128)S(1)} %bitcast.148, pred[2048,1024]{0,1:T(8,128)(4,1)S(1)} %compare_and_fusion, f32[2048,1,2,128]{0,3,2,1:T(8,128)S(1)} %get-tuple-element.261, f32[2048,2]{0,1:T(2,128)S(1)} %get-tuple-element.726, ...), kind=kOutput, calls=%fused_computation.12 | convolution fusion | flops 1095761920 | bytes 23364096 | tf_op jit(solution)/shard_map/while/body/eval_jaxpr/while/body/eval_jaxpr/cond/branch_1_fun/qgmk,kgd->qgmd/dot_general | solution.py:42
  131.5 18.0 %conditional.3 = ((f32[2048,1,2]{0,2,1:T(2,128)S(1)}, f32[2048,1,2]{0,2,1:T(2,128)S(1)}, f32[2048,1,2,128]{0,3,2,1:T(8,128)S(1)})) conditional(s32[]{:T(128)} %convert_element_type.42, (f32[2048,1,2]{0,2,1:T(2,128)S(1)}, f32[2048,1,2]{0,2,1:T(2,128)S(1)}, f32[2048,1,2,128]{0,3,2,1:T(8,128)S(1)}) %tuple.146, (s32[]{:T(128)}, s32[]{:T(128)}, s32[]{:T(128)}, ...), branch_computations={%region_2.1_spmd, %region_3.4_spmd} | conditional | flops 2207269888 | bytes 64785456 | solution.py:65
  131.6 1.7 compare_and_fusion
  133.3 4.6 %fusion.2 = (f32[2048,2]{0,1:T(2,128)S(1)}, f32[1024,2048,2]{1,0,2:T(8,128)S(1)}) fusion(pred[2048,1024]{0,1:T(8,128)(4,1)S(1)} %compare_and_fusion, bf16[2048,1,2,128]{3,0,2,1:T(8,128)(2,1)S(1)} %get-tuple-element.259, bf16[4,1024,1,128]{3,1,2,0:T(8,128)(2,1)} %get-tuple-element.257, s32[]{:T(128)} %get-tuple-element.258), kind=kOutput, calls=%fused_computation.4 | convolution fusion | flops 1086320640 | bytes 20201984 | tf_op jit(solution)/shard_map/while/body/eval_jaxpr/while/body/eval_jaxpr/cond/branch_1_fun/qgmd,kgd->qgmk/dot_general | solution.py:30
  137.9 4.5 %fusion.4 = f32[2048,2]{0,1:T(2,128)S(1)} fusion(f32[1024,2048,2]{1,0,2:T(8,128)S(1)} %get-tuple-element.729, f32[2048,2]{0,1:T(2,128)S(1)} %bitcast.147, pred[2048,1024]{0,1:T(8,128)(4,1)S(1)} %compare_and_fusion), kind=kLoop, calls=%fused_computation.6 | loop fusion | flops 20967424 | bytes 18907136 | tf_op jit(solution)/shard_map/while/body/eval_jaxpr/while/body/eval_jaxpr/cond/branch_1_fun/reduce_sum | solution.py:41
  142.5 7.1 %fusion.12 = f32[2048,1,2,128]{0,3,2,1:T(8,128)S(1)} fusion(f32[1024,2048,2]{1,0,2:T(8,128)S(1)} %get-tuple-element.729, f32[2048,2]{0,1:T(2,128)S(1)} %bitcast.148, pred[2048,1024]{0,1:T(8,128)(4,1)S(1)} %compare_and_fusion, f32[2048,1,2,128]{0,3,2,1:T(8,128)S(1)} %get-tuple-element.261, f32[2048,2]{0,1:T(2,128)S(1)} %get-tuple-element.726, ...), kind=kOutput, calls=%fused_computation.12 | convolution fusion | flops 1095761920 | bytes 23364096 | tf_op jit(solution)/shard_map/while/body/eval_jaxpr/while/body/eval_jaxpr/cond/branch_1_fun/qgmk,kgd->qgmd/dot_general | solution.py:42
  156.8 2.3 copy.352
  159.3 77.5 %while.55 = (s32[]{:T(128)}, f32[2048,1,2]{0,2,1:T(2,128)S(1)}, f32[2048,1,2]{0,2,1:T(2,128)S(1)}, f32[2048,1,2,128]{0,3,2,1:T(8,128)S(1)}, s32[4]{0:T(128)S(1)}...) while((s32[]{:T(128)}, f32[2048,1,2]{0,2,1:T(2,128)S(1)}, ...), condition=%wide.region_6.6_spmd.clone, body=%wide.region_1.5_spmd.clone.sunk | while | flops 2207269888 | bytes 64793944 | solution.py:75
  160.6 18.0 %conditional.3 = ((f32[2048,1,2]{0,2,1:T(2,128)S(1)}, f32[2048,1,2]{0,2,1:T(2,128)S(1)}, f32[2048,1,2,128]{0,3,2,1:T(8,128)S(1)})) conditional(s32[]{:T(128)} %convert_element_type.42, (f32[2048,1,2]{0,2,1:T(2,128)S(1)}, f32[2048,1,2]{0,2,1:T(2,128)S(1)}, f32[2048,1,2,128]{0,3,2,1:T(8,128)S(1)}) %tuple.146, (s32[]{:T(128)}, s32[]{:T(128)}, s32[]{:T(128)}, ...), branch_computations={%region_2.1_spmd, %region_3.4_spmd} | conditional | flops 2207269888 | bytes 64785456 | solution.py:65
  160.7 1.7 compare_and_fusion
  162.4 4.6 %fusion.2 = (f32[2048,2]{0,1:T(2,128)S(1)}, f32[1024,2048,2]{1,0,2:T(8,128)S(1)}) fusion(pred[2048,1024]{0,1:T(8,128)(4,1)S(1)} %compare_and_fusion, bf16[2048,1,2,128]{3,0,2,1:T(8,128)(2,1)S(1)} %get-tuple-element.259, bf16[4,1024,1,128]{3,1,2,0:T(8,128)(2,1)} %get-tuple-element.257, s32[]{:T(128)} %get-tuple-element.258), kind=kOutput, calls=%fused_computation.4 | convolution fusion | flops 1086320640 | bytes 20201984 | tf_op jit(solution)/shard_map/while/body/eval_jaxpr/while/body/eval_jaxpr/cond/branch_1_fun/qgmd,kgd->qgmk/dot_general | solution.py:30
  167.0 4.5 %fusion.4 = f32[2048,2]{0,1:T(2,128)S(1)} fusion(f32[1024,2048,2]{1,0,2:T(8,128)S(1)} %get-tuple-element.729, f32[2048,2]{0,1:T(2,128)S(1)} %bitcast.147, pred[2048,1024]{0,1:T(8,128)(4,1)S(1)} %compare_and_fusion), kind=kLoop, calls=%fused_computation.6 | loop fusion | flops 20967424 | bytes 18907136 | tf_op jit(solution)/shard_map/while/body/eval_jaxpr/while/body/eval_jaxpr/cond/branch_1_fun/reduce_sum | solution.py:41
  171.6 7.1 %fusion.12 = f32[2048,1,2,128]{0,3,2,1:T(8,128)S(1)} fusion(f32[1024,2048,2]{1,0,2:T(8,128)S(1)} %get-tuple-element.729, f32[2048,2]{0,1:T(2,128)S(1)} %bitcast.148, pred[2048,1024]{0,1:T(8,128)(4,1)S(1)} %compare_and_fusion, f32[2048,1,2,128]{0,3,2,1:T(8,128)S(1)} %get-tuple-element.261, f32[2048,2]{0,1:T(2,128)S(1)} %get-tuple-element.726, ...), kind=kOutput, calls=%fused_computation.12 | convolution fusion | flops 1095761920 | bytes 23364096 | tf_op jit(solution)/shard_map/while/body/eval_jaxpr/while/body/eval_jaxpr/cond/branch_1_fun/qgmk,kgd->qgmd/dot_general | solution.py:42
  180.0 18.0 %conditional.3 = ((f32[2048,1,2]{0,2,1:T(2,128)S(1)}, f32[2048,1,2]{0,2,1:T(2,128)S(1)}, f32[2048,1,2,128]{0,3,2,1:T(8,128)S(1)})) conditional(s32[]{:T(128)} %convert_element_type.42, (f32[2048,1,2]{0,2,1:T(2,128)S(1)}, f32[2048,1,2]{0,2,1:T(2,128)S(1)}, f32[2048,1,2,128]{0,3,2,1:T(8,128)S(1)}) %tuple.146, (s32[]{:T(128)}, s32[]{:T(128)}, s32[]{:T(128)}, ...), branch_computations={%region_2.1_spmd, %region_3.4_spmd} | conditional | flops 2207269888 | bytes 64785456 | solution.py:65
  180.0 1.7 compare_and_fusion
  181.8 4.6 %fusion.2 = (f32[2048,2]{0,1:T(2,128)S(1)}, f32[1024,2048,2]{1,0,2:T(8,128)S(1)}) fusion(pred[2048,1024]{0,1:T(8,128)(4,1)S(1)} %compare_and_fusion, bf16[2048,1,2,128]{3,0,2,1:T(8,128)(2,1)S(1)} %get-tuple-element.259, bf16[4,1024,1,128]{3,1,2,0:T(8,128)(2,1)} %get-tuple-element.257, s32[]{:T(128)} %get-tuple-element.258), kind=kOutput, calls=%fused_computation.4 | convolution fusion | flops 1086320640 | bytes 20201984 | tf_op jit(solution)/shard_map/while/body/eval_jaxpr/while/body/eval_jaxpr/cond/branch_1_fun/qgmd,kgd->qgmk/dot_general | solution.py:30
  186.4 4.5 %fusion.4 = f32[2048,2]{0,1:T(2,128)S(1)} fusion(f32[1024,2048,2]{1,0,2:T(8,128)S(1)} %get-tuple-element.729, f32[2048,2]{0,1:T(2,128)S(1)} %bitcast.147, pred[2048,1024]{0,1:T(8,128)(4,1)S(1)} %compare_and_fusion), kind=kLoop, calls=%fused_computation.6 | loop fusion | flops 20967424 | bytes 18907136 | tf_op jit(solution)/shard_map/while/body/eval_jaxpr/while/body/eval_jaxpr/cond/branch_1_fun/reduce_sum | solution.py:41
  191.0 7.1 %fusion.12 = f32[2048,1,2,128]{0,3,2,1:T(8,128)S(1)} fusion(f32[1024,2048,2]{1,0,2:T(8,128)S(1)} %get-tuple-element.729, f32[2048,2]{0,1:T(2,128)S(1)} %bitcast.148, pred[2048,1024]{0,1:T(8,128)(4,1)S(1)} %compare_and_fusion, f32[2048,1,2,128]{0,3,2,1:T(8,128)S(1)} %get-tuple-element.261, f32[2048,2]{0,1:T(2,128)S(1)} %get-tuple-element.726, ...), kind=kOutput, calls=%fused_computation.12 | convolution fusion | flops 1095761920 | bytes 23364096 | tf_op jit(solution)/shard_map/while/body/eval_jaxpr/while/body/eval_jaxpr/cond/branch_1_fun/qgmk,kgd->qgmd/dot_general | solution.py:42
  199.4 18.0 %conditional.3 = ((f32[2048,1,2]{0,2,1:T(2,128)S(1)}, f32[2048,1,2]{0,2,1:T(2,128)S(1)}, f32[2048,1,2,128]{0,3,2,1:T(8,128)S(1)})) conditional(s32[]{:T(128)} %convert_element_type.42, (f32[2048,1,2]{0,2,1:T(2,128)S(1)}, f32[2048,1,2]{0,2,1:T(2,128)S(1)}, f32[2048,1,2,128]{0,3,2,1:T(8,128)S(1)}) %tuple.146, (s32[]{:T(128)}, s32[]{:T(128)}, s32[]{:T(128)}, ...), branch_computations={%region_2.1_spmd, %region_3.4_spmd} | conditional | flops 2207269888 | bytes 64785456 | solution.py:65
  199.4 1.7 compare_and_fusion
  201.1 4.6 %fusion.2 = (f32[2048,2]{0,1:T(2,128)S(1)}, f32[1024,2048,2]{1,0,2:T(8,128)S(1)}) fusion(pred[2048,1024]{0,1:T(8,128)(4,1)S(1)} %compare_and_fusion, bf16[2048,1,2,128]{3,0,2,1:T(8,128)(2,1)S(1)} %get-tuple-element.259, bf16[4,1024,1,128]{3,1,2,0:T(8,128)(2,1)} %get-tuple-element.257, s32[]{:T(128)} %get-tuple-element.258), kind=kOutput, calls=%fused_computation.4 | convolution fusion | flops 1086320640 | bytes 20201984 | tf_op jit(solution)/shard_map/while/body/eval_jaxpr/while/body/eval_jaxpr/cond/branch_1_fun/qgmd,kgd->qgmk/dot_general | solution.py:30
  205.8 4.5 %fusion.4 = f32[2048,2]{0,1:T(2,128)S(1)} fusion(f32[1024,2048,2]{1,0,2:T(8,128)S(1)} %get-tuple-element.729, f32[2048,2]{0,1:T(2,128)S(1)} %bitcast.147, pred[2048,1024]{0,1:T(8,128)(4,1)S(1)} %compare_and_fusion), kind=kLoop, calls=%fused_computation.6 | loop fusion | flops 20967424 | bytes 18907136 | tf_op jit(solution)/shard_map/while/body/eval_jaxpr/while/body/eval_jaxpr/cond/branch_1_fun/reduce_sum | solution.py:41
  210.3 7.1 %fusion.12 = f32[2048,1,2,128]{0,3,2,1:T(8,128)S(1)} fusion(f32[1024,2048,2]{1,0,2:T(8,128)S(1)} %get-tuple-element.729, f32[2048,2]{0,1:T(2,128)S(1)} %bitcast.148, pred[2048,1024]{0,1:T(8,128)(4,1)S(1)} %compare_and_fusion, f32[2048,1,2,128]{0,3,2,1:T(8,128)S(1)} %get-tuple-element.261, f32[2048,2]{0,1:T(2,128)S(1)} %get-tuple-element.726, ...), kind=kOutput, calls=%fused_computation.12 | convolution fusion | flops 1095761920 | bytes 23364096 | tf_op jit(solution)/shard_map/while/body/eval_jaxpr/while/body/eval_jaxpr/cond/branch_1_fun/qgmk,kgd->qgmd/dot_general | solution.py:42
  218.7 18.0 %conditional.3 = ((f32[2048,1,2]{0,2,1:T(2,128)S(1)}, f32[2048,1,2]{0,2,1:T(2,128)S(1)}, f32[2048,1,2,128]{0,3,2,1:T(8,128)S(1)})) conditional(s32[]{:T(128)} %convert_element_type.42, (f32[2048,1,2]{0,2,1:T(2,128)S(1)}, f32[2048,1,2]{0,2,1:T(2,128)S(1)}, f32[2048,1,2,128]{0,3,2,1:T(8,128)S(1)}) %tuple.146, (s32[]{:T(128)}, s32[]{:T(128)}, s32[]{:T(128)}, ...), branch_computations={%region_2.1_spmd, %region_3.4_spmd} | conditional | flops 2207269888 | bytes 64785456 | solution.py:65
  220.5 4.6 %fusion.2 = (f32[2048,2]{0,1:T(2,128)S(1)}, f32[1024,2048,2]{1,0,2:T(8,128)S(1)}) fusion(pred[2048,1024]{0,1:T(8,128)(4,1)S(1)} %compare_and_fusion, bf16[2048,1,2,128]{3,0,2,1:T(8,128)(2,1)S(1)} %get-tuple-element.259, bf16[4,1024,1,128]{3,1,2,0:T(8,128)(2,1)} %get-tuple-element.257, s32[]{:T(128)} %get-tuple-element.258), kind=kOutput, calls=%fused_computation.4 | convolution fusion | flops 1086320640 | bytes 20201984 | tf_op jit(solution)/shard_map/while/body/eval_jaxpr/while/body/eval_jaxpr/cond/branch_1_fun/qgmd,kgd->qgmk/dot_general | solution.py:30
  225.1 4.5 %fusion.4 = f32[2048,2]{0,1:T(2,128)S(1)} fusion(f32[1024,2048,2]{1,0,2:T(8,128)S(1)} %get-tuple-element.729, f32[2048,2]{0,1:T(2,128)S(1)} %bitcast.147, pred[2048,1024]{0,1:T(8,128)(4,1)S(1)} %compare_and_fusion), kind=kLoop, calls=%fused_computation.6 | loop fusion | flops 20967424 | bytes 18907136 | tf_op jit(solution)/shard_map/while/body/eval_jaxpr/while/body/eval_jaxpr/cond/branch_1_fun/reduce_sum | solution.py:41
  229.7 7.1 %fusion.12 = f32[2048,1,2,128]{0,3,2,1:T(8,128)S(1)} fusion(f32[1024,2048,2]{1,0,2:T(8,128)S(1)} %get-tuple-element.729, f32[2048,2]{0,1:T(2,128)S(1)} %bitcast.148, pred[2048,1024]{0,1:T(8,128)(4,1)S(1)} %compare_and_fusion, f32[2048,1,2,128]{0,3,2,1:T(8,128)S(1)} %get-tuple-element.261, f32[2048,2]{0,1:T(2,128)S(1)} %get-tuple-element.726, ...), kind=kOutput, calls=%fused_computation.12 | convolution fusion | flops 1095761920 | bytes 23364096 | tf_op jit(solution)/shard_map/while/body/eval_jaxpr/while/body/eval_jaxpr/cond/branch_1_fun/qgmk,kgd->qgmd/dot_general | solution.py:42
  238.8 3.1 %copy.310 = bf16[8,512,2,128]{3,1,2,0:T(8,128)(2,1)} copy(bf16[8,512,2,128]{3,1,0,2:T(8,128)(2,1)} %bitcast.161) | data formatting | bytes 4194304 | tf_op jit(solution)/shard_map/reshape | solution.py:150
  241.9 7.2 %all-to-all-start.1 = ((bf16[8,512,2,128]{3,1,2,0:T(8,128)(2,1)}), bf16[8,512,2,128]{3,1,2,0:T(8,128)(2,1)S(1)}, u32[]{:S(2)}, u32[]{:S(2)}) async-start(bf16[8,512,2,128]{3,1,2,0:T(8,128)(2,1)} %copy.310), calls=%async_computation.1 | async-start | bytes 4194304 | tf_op jit(solution)/shard_map/all_to_all | solution.py:151
  249.1 2.3 copy.313
  251.4 23.7 %all-to-all-done.1 = bf16[8,512,2,128]{3,1,2,0:T(8,128)(2,1)S(1)} async-done(((bf16[8,512,2,128]{3,1,2,0:T(8,128)(2,1)}), bf16[8,512,2,128]{3,1,2,0:T(8,128)(2,1)S(1)}, u32[]{:S(2)}, u32[]{:S(2)}) %all-to-all-start.1) | async-done | bytes 2097184 | tf_op jit(solution)/shard_map/all_to_all | solution.py:151
  275.2 2.7 copy.312
  (115 shorter events, 35.2 us)
Async XLA Ops:
  6.5 19.4 %copy-start = (bf16[512,4,128]{2,1,0:T(4,128)(2,1)S(1)}, bf16[512,4,128]{2,1,0:T(4,128)(2,1)}, u32[]{:S(2)}) copy-start(bf16[512,4,128]{2,1,0:T(4,128)(2,1)} %param.13) | copy-start | bytes 1572868
  8.0 18.0 %copy-start.1 = (bf16[512,4,128]{2,1,0:T(4,128)(2,1)S(1)}, bf16[512,4,128]{2,1,0:T(4,128)(2,1)}, u32[]{:S(2)}) copy-start(bf16[512,4,128]{2,1,0:T(4,128)(2,1)} %param.12) | copy-start | bytes 1572868
  19.5 20.3 %all-to-all-start.2 = ((bf16[16,1,2,128,1,128]{5,3,2,4,1,0:T(8,128)(2,1)}), bf16[16,1,2,128,1,128]{5,3,2,4,1,0:T(8,128)(2,1)S(1)}, u32[]{:S(2)}, u32[]{:S(2)}) async-start(bf16[16,1,2,128,1,128]{5,3,2,4,1,0:T(8,128)(2,1)} %bitcast_dynamic-update-slice_fusion), calls=%async_computation.2 | async-start | bytes 2097152 | tf_op jit(solution)/shard_map/all_to_all | solution.py:106
  30.7 15.7 %copy-start.2 = (s32[16]{0:T(128)S(1)}, s32[16]{0:T(128)}, u32[]{:S(2)}) copy-start(s32[16]{0:T(128)} %param.15) | copy-start | bytes 196
  39.8 55.9 %all-to-all-start = ((bf16[512,8,4,128]{3,0,2,1:T(8,128)(2,1)}), bf16[512,8,4,128]{3,0,2,1:T(8,128)(2,1)}, u32[]{:S(2)}, u32[]{:S(2)}) async-start(bf16[512,8,4,128]{3,0,2,1:T(8,128)(2,1)} %pad_maximum_fusion), calls=%async_computation | async-start | bytes 8388608 | tf_op jit(solution)/shard_map/all_to_all | solution.py:13
  95.6 146.3 %all-to-all-start.3 = ((bf16[16,2,1,1,128,128]{5,4,1,3,2,0:T(8,128)(2,1)}), bf16[16,2,1,1,128,128]{5,4,1,3,2,0:T(8,128)(2,1)}, u32[]{:S(2)}, u32[]{:S(2)}) async-start(bf16[16,2,1,1,128,128]{5,4,1,3,2,0:T(8,128)(2,1)} %fusion.28), calls=%async_computation.3 | async-start | bytes 2097152 | tf_op jit(solution)/shard_map/all_to_all | solution.py:113
  241.9 33.2 %all-to-all-start.1 = ((bf16[8,512,2,128]{3,1,2,0:T(8,128)(2,1)}), bf16[8,512,2,128]{3,1,2,0:T(8,128)(2,1)S(1)}, u32[]{:S(2)}, u32[]{:S(2)}) async-start(bf16[8,512,2,128]{3,1,2,0:T(8,128)(2,1)} %copy.310), calls=%async_computation.1 | async-start | bytes 4194304 | tf_op jit(solution)/shard_map/all_to_all | solution.py:151
